TPU v7x, 32 devices: a whole 2x2x4 slice. The times are simulated.
32 devices in a mesh: cond: 2 (over x), gx: 4 (over y, core), yz: 4 (over z).
Axes of the slice: x: 2, y: 2, z: 4, core: 2. Of those that a mesh axis runs over, the one named last changes fastest.
Arguments:
- adjoint: float32 [2, 5, 32, 64, 256], P('cond', None, 'gx', 'yz'), may hold values from -6 to 6
- objective_gradient: float32 [2, 5, 32, 64, 256], P('cond', None, 'gx', 'yz'), may hold values from -6 to 6
- diagonal: float32 [32, 64, 256], P('gx', 'yz'), may hold values from 4 to 12
- flux_blocks: float32 [2, 6, 5, 5], P('cond'), may hold values from -1 to 1
- flux_sensitivity: bfloat16 [2, 5, 32, 64, 256], P('cond', None, 'gx', 'yz'), may hold values from -6 to 6
- surface_mask: int32 [32, 64, 256], P('gx', 'yz'), may hold values 0 or 1
- patch_band_slot: int32 [32, 64], P('gx', 'yz'), may hold values from 0 to 62
- design_basis: float32 [256, 128], replicated, may hold values from -0.046875 to 0.046875
- condition_weights: int32 [2], replicated, may hold values from 1 to 999, as said below
Outputs:
- smoothed: float32 [2, 5, 32, 64, 256], P('cond', None, 'gx', 'yz')
- residual: float32 [2, 5, 32, 64, 256], P('cond', None, 'gx', 'yz')
- design_gradient: float32 [4096], P(('gx', 'yz'))
Inputs may be any that keep to these rules, and one draw needn't show every extreme that they name: `condition_weights`: positive integer weights; one condition has weight 999.
All inputs are finite; a program needn't handle non-finite values. No bound on the sum of `surface_mask` on one device may be relied on, other than what follows from the above.
Results may differ from a plain program's by a relative error of at most 0.0003.
Values sent between devices are 32-bit elements; how exact they have to be, the bound alone decides.
A program may use at most 64 MiB of HBM per device.

v0:
```python
import jax
import jax.numpy as jnp
from jax import lax
from jax.sharding import PartitionSpec as P

NDES = 4096
relaxation = 0.8
neighbour_starts = ((2, 1, 1), (0, 1, 1), (1, 2, 1), (1, 0, 1), (1, 1, 2), (1, 1, 0))


def with_halo(block, sides, width):
    for axis, dim in sides:
        count = lax.axis_size(axis)
        forward = [(i, i + 1) for i in range(count - 1)]
        backward = [(target, source) for source, target in forward]
        low = lax.ppermute(
            lax.slice_in_dim(block, block.shape[dim] - width, None, axis=dim), axis, forward
        )
        high = lax.ppermute(lax.slice_in_dim(block, 0, width, axis=dim), axis, backward)
        block = jnp.concatenate([low, block, high], axis=dim)
    return block


def apply_operator(padded_field, diagonal, blocks):
    size_x = padded_field.shape[1] - 2
    size_y = padded_field.shape[2] - 2
    size_z = padded_field.shape[3] - 2
    result = diagonal * padded_field[:, 1:-1, 1:-1, 1:-1]
    for direction in range(6):
        start_x, start_y, start_z = neighbour_starts[direction]
        shifted = padded_field[
            :, start_x : start_x + size_x, start_y : start_y + size_y, start_z : start_z + size_z
        ]
        result = result - jnp.einsum(
            "ec,exyz->cxyz", blocks[direction], shifted, precision=lax.Precision.HIGHEST
        )
    return result


def spread_bands(slot_lookup):
    halfway = slot_lookup.shape[1] // 2
    first_half = jnp.pad(slot_lookup[:, :halfway], ((0, 1), (0, 0)))
    second_half = jnp.pad(slot_lookup[:, halfway:], ((1, 0), (0, 0)))
    return (first_half + second_half).reshape(-1)


def pad_third(values):
    return jnp.pad(values, ((0, 0), (0, 0), (0, 0), (1, 1)))


def local(
    adjoint,
    objective_gradient,
    diagonal,
    flux_blocks,
    flux_sensitivity,
    surface_mask,
    patch_band_slot,
    design_basis,
    condition_weights,
):
    blocks = flux_blocks[0]
    source = objective_gradient[0]
    start_field = adjoint[0]

    def operate(values):
        haloed = with_halo(values, (("gx", 1), ("yz", 2)), 1)
        return apply_operator(pad_third(haloed), diagonal, blocks)

    relaxed = start_field + relaxation * (source - operate(start_field)) / diagonal
    smoothed = relaxed + relaxation * (source - operate(relaxed)) / diagonal
    residual = source - operate(smoothed)
    surface = surface_mask.astype(jnp.float32) * jnp.sum(
        smoothed * flux_sensitivity[0].astype(jnp.float32), axis=0
    )
    projected_gradient = jnp.dot(
        surface.reshape(-1, surface.shape[-1]),
        design_basis,
        precision=lax.Precision.HIGHEST,
        preferred_element_type=jnp.float32,
    )
    slot_count = 2 * NDES // design_basis.shape[1] - 1
    onehot = (jnp.arange(slot_count)[:, None] == patch_band_slot.reshape(1, -1)).astype(jnp.float32)
    slot_lookup = jnp.dot(
        onehot,
        projected_gradient,
        precision=lax.Precision.HIGHEST,
        preferred_element_type=jnp.float32,
    )
    gradient = spread_bands(slot_lookup)
    weights_float = condition_weights.astype(jnp.float32)
    picked = jnp.arange(weights_float.shape[0]) == lax.axis_index("cond")
    local_portion = jnp.sum(jnp.where(picked, weights_float, 0.0)) / jnp.sum(weights_float)
    summed = lax.psum(local_portion * gradient, ("cond", "gx", "yz"))
    pieces = NDES // lax.axis_size(("gx", "yz"))
    design_gradient = lax.dynamic_slice_in_dim(
        summed, lax.axis_index(("gx", "yz")) * pieces, pieces, 0
    )
    return (smoothed[None], residual[None], design_gradient)


def solution(mesh):
    placed = (
        P("cond", None, "gx", "yz", None),
        P("cond", None, "gx", "yz", None),
        P("gx", "yz", None),
        P("cond", None, None, None),
        P("cond", None, "gx", "yz", None),
        P("gx", "yz", None),
        P("gx", "yz"),
        P(),
        P(),
    )
    return jax.shard_map(
        local,
        mesh=mesh,
        in_specs=placed,
        out_specs=(
            P("cond", None, "gx", "yz", None),
            P("cond", None, "gx", "yz", None),
            P(("gx", "yz")),
        ),
        check_vma=False,
    )
```

profile of v0, /device:TPU:12, one launch (start us, length us, event | category | flops | bytes accessed | tf_op | source)
XLA Modules:
  0.0 115.4 jit_solution(11190379338171602337)
XLA Ops:
  0.6 0.0 copy-start
  0.7 1.5 %copy.88 = f32[1,5,8,16,256]{4,1,3,2,0:T(8,128)S(1)} copy(f32[1,5,8,16,256]{4,3,2,1,0:T(8,128)} %param.9) | data formatting | bytes 1310720 | tf_op args[0]
  2.2 1.9 %collective-permute-start = (f32[5,1,16,256]{3,0,2,1:T(8,128)S(1)}, f32[5,1,16,256]{3,0,2,1:T(8,128)S(1)}, u32[]{:S(2)}, u32[]{:S(2)}) collective-permute-start(f32[5,1,16,256]{3,0,2,1:T(8,128)S(1)} %get-tuple-element.19), channel_id=1, source_target_pairs={{4,0},{8,4},{12,8},{5,1},{9,5},{13,9},{6,2},{10,6},{14,10},{7,3},{... | collective-permute-start | bytes 245768 | tf_op jit(solution)/shard_map/ppermute | solution.py:19
  4.1 2.4 %collective-permute-start.1 = (f32[5,1,16,256]{3,0,2,1:T(8,128)S(1)}, f32[5,1,16,256]{3,0,2,1:T(8,128)S(1)}, u32[]{:S(2)}, u32[]{:S(2)}) collective-permute-start(f32[5,1,16,256]{3,0,2,1:T(8,128)S(1)} %get-tuple-element.18), channel_id=1, source_target_pairs={{0,4},{4,8},{8,12},{1,5},{5,9},{9,13},{2,6},{6,10},{10,14},{3,7},{... | collective-permute-start | bytes 245768 | tf_op jit(solution)/shard_map/ppermute | solution.py:16
  6.6 0.2 fusion.157
  6.8 0.1 copy.82
  6.9 0.1 copy.81
  7.0 0.1 copy.80
  7.2 0.1 copy.79
  7.3 0.1 copy.78
  7.4 0.1 copy.77
  7.6 0.1 eq.24
  7.6 0.0 collective-permute-done
  7.7 2.8 %collective-permute-done.1 = f32[5,1,16,256]{3,0,2,1:T(8,128)S(1)} collective-permute-done((f32[5,1,16,256]{3,0,2,1:T(8,128)S(1)}, f32[5,1,16,256]{3,0,2,1:T(8,128)S(1)}, u32[]{:S(2)}, u32[]{:S(2)}) %collective-permute-start.1) | collective-permute-done | bytes 81952 | tf_op jit(solution)/shard_map/ppermute | solution.py:16
  10.4 2.4 %collective-permute-start.2 = (f32[5,10,1,256]{3,0,2,1:T(8,128)S(1)}, f32[5,10,1,256]{3,0,2,1:T(8,128)S(1)}, u32[]{:S(2)}, u32[]{:S(2)}) collective-permute-start(f32[5,10,1,256]{3,0,2,1:T(8,128)S(1)} %get-tuple-element.13), channel_id=1, source_target_pairs={{1,0},{2,1},{3,2},{5,4},{6,5},{7,6},{9,8},{10,9},{11,10},{13,12},{... | collective-permute-start | bytes 153608 | tf_op jit(solution)/shard_map/ppermute | solution.py:19
  12.8 3.5 %collective-permute-start.3 = (f32[5,10,1,256]{3,0,2,1:T(8,128)S(1)}, f32[5,10,1,256]{3,0,2,1:T(8,128)S(1)}, u32[]{:S(2)}, u32[]{:S(2)}) collective-permute-start(f32[5,10,1,256]{3,0,2,1:T(8,128)S(1)} %get-tuple-element.12), channel_id=1, source_target_pairs={{0,1},{1,2},{2,3},{4,5},{5,6},{6,7},{8,9},{9,10},{10,11},{12,13},{... | collective-permute-start | bytes 153608 | tf_op jit(solution)/shard_map/ppermute | solution.py:16
  16.3 1.1 convolution_bitcast_fusion.4
  17.4 0.0 collective-permute-done.2
  17.4 1.8 %collective-permute-done.3 = f32[5,10,1,256]{3,0,2,1:T(8,128)S(1)} collective-permute-done((f32[5,10,1,256]{3,0,2,1:T(8,128)S(1)}, f32[5,10,1,256]{3,0,2,1:T(8,128)S(1)}, u32[]{:S(2)}, u32[]{:S(2)}) %collective-permute-start.3) | collective-permute-done | bytes 51232 | tf_op jit(solution)/shard_map/ppermute | solution.py:16
  19.1 0.6 select_maximum_fusion.8
  19.8 1.0 convolution_bitcast_fusion.10
  20.9 1.2 %convolution_bitcast_fusion.11 = f32[5,8,16,256]{3,0,2,1:T(8,128)S(1)} fusion(f32[5,10,18,258]{3,0,2,1:T(8,128)S(1)} %select_maximum_fusion.8, f32[1,1,5,5]{3,2,1,0:T(8,128)S(1)} %copy.81), kind=kOutput, calls=%fused_computation.86 | convolution fusion | flops 9830400 | bytes 1708032 | tf_op jit(solution)/shard_map/ec,exyz->cxyz/dot_general | solution.py:34
  22.1 0.0 copy-start.1
  22.1 0.0 copy-start.2
  22.1 1.1 fusion.61
  23.2 1.1 fusion.64
  24.3 0.0 copy-start.7
  24.3 2.0 %fusion.94 = f32[5,8,16,256]{3,0,2,1:T(8,128)S(1)} fusion(f32[5,8,16,256]{3,0,2,1:T(8,128)S(1)} %bitcast.184, f32[5,8,16,256]{3,0,2,1:T(8,128)S(1)} %convolution_bitcast_fusion.10, f32[5,8,16,256]{3,0,2,1:T(8,128)S(1)} %convolution_bitcast_fusion.11, f32[5,8,16,256]{3,0,2,1:T(8,128)S(1)} %fusion.61, f32[5,8,16,256]{3,0,2,1:T(8,128)S(1)} %fusion.64, ...), kind=kOutput, calls=%fused_computation.108 | convolution fusion | flops 11816960 | bytes 5455972 | tf_op jit(solution)/shard_map/ec,exyz->cxyz/dot_general | solution.py:34
  26.3 1.9 %collective-permute-start.4 = (f32[5,1,16,256]{3,0,2,1:T(8,128)S(1)}, f32[5,1,16,256]{3,0,2,1:T(8,128)S(1)}, u32[]{:S(2)}, u32[]{:S(2)}) collective-permute-start(f32[5,1,16,256]{3,0,2,1:T(8,128)S(1)} %get-tuple-element.17), channel_id=1, source_target_pairs={{4,0},{8,4},{12,8},{5,1},{9,5},{13,9},{6,2},{10,6},{14,10},{7,3},{... | collective-permute-start | bytes 245768 | tf_op jit(solution)/shard_map/ppermute | solution.py:19
  28.3 2.4 %collective-permute-start.5 = (f32[5,1,16,256]{3,0,2,1:T(8,128)S(1)}, f32[5,1,16,256]{3,0,2,1:T(8,128)S(1)}, u32[]{:S(2)}, u32[]{:S(2)}) collective-permute-start(f32[5,1,16,256]{3,0,2,1:T(8,128)S(1)} %get-tuple-element.16), channel_id=1, source_target_pairs={{0,4},{4,8},{8,12},{1,5},{5,9},{9,13},{2,6},{6,10},{10,14},{3,7},{... | collective-permute-start | bytes 245768 | tf_op jit(solution)/shard_map/ppermute | solution.py:16
  30.7 0.6 convert_reduce_fusion
  32.7 1.9 %collective-permute-done.5 = f32[5,1,16,256]{3,0,2,1:T(8,128)S(1)} collective-permute-done((f32[5,1,16,256]{3,0,2,1:T(8,128)S(1)}, f32[5,1,16,256]{3,0,2,1:T(8,128)S(1)}, u32[]{:S(2)}, u32[]{:S(2)}) %collective-permute-start.5) | collective-permute-done | bytes 81952 | tf_op jit(solution)/shard_map/ppermute | solution.py:16
  34.6 1.9 %collective-permute-start.6 = (f32[5,10,1,256]{3,0,2,1:T(8,128)S(1)}, f32[5,10,1,256]{3,0,2,1:T(8,128)S(1)}, u32[]{:S(2)}, u32[]{:S(2)}) collective-permute-start(f32[5,10,1,256]{3,0,2,1:T(8,128)S(1)} %get-tuple-element.11), channel_id=1, source_target_pairs={{1,0},{2,1},{3,2},{5,4},{6,5},{7,6},{9,8},{10,9},{11,10},{13,12},{... | collective-permute-start | bytes 153608 | tf_op jit(solution)/shard_map/ppermute | solution.py:19
  36.5 4.1 %collective-permute-start.7 = (f32[5,10,1,256]{3,0,2,1:T(8,128)S(1)}, f32[5,10,1,256]{3,0,2,1:T(8,128)S(1)}, u32[]{:S(2)}, u32[]{:S(2)}) collective-permute-start(f32[5,10,1,256]{3,0,2,1:T(8,128)S(1)} %get-tuple-element.10), channel_id=1, source_target_pairs={{0,1},{1,2},{2,3},{4,5},{5,6},{6,7},{8,9},{9,10},{10,11},{12,13},{... | collective-permute-start | bytes 153608 | tf_op jit(solution)/shard_map/ppermute | solution.py:16
  40.6 1.1 convolution_bitcast_fusion.2
  41.7 1.1 collective-permute-done.7
  42.8 0.6 select_maximum_fusion.4
  43.5 1.0 convolution_bitcast_fusion.8
  44.5 1.2 %convolution_bitcast_fusion.9 = f32[5,8,16,256]{3,0,2,1:T(8,128)S(1)} fusion(f32[5,10,18,258]{3,0,2,1:T(8,128)S(1)} %select_maximum_fusion.4, f32[1,1,5,5]{3,2,1,0:T(8,128)S(1)} %copy.81), kind=kOutput, calls=%fused_computation.84 | convolution fusion | flops 9830400 | bytes 1708032 | tf_op jit(solution)/shard_map/ec,exyz->cxyz/dot_general | solution.py:34
  45.8 0.0 copy-start.3
  45.8 1.1 fusion.55
  46.9 1.1 fusion.58
  47.9 2.2 %fusion.119 = (f32[8,16,256]{2,1,0:T(8,128)S(1)}, f32[5,8,16,256]{3,0,2,1:T(8,128)S(1)}) fusion(bf16[1,5,8,16,256]{4,3,2,1,0:T(8,128)(2,1)S(1)} %copy-done.3, f32[5,8,16,256]{3,0,2,1:T(8,128)S(1)} %fusion.94, f32[5,8,16,256]{3,0,2,1:T(8,128)S(1)} %convolution_bitcast_fusion.8, f32[5,8,16,256]{3,0,2,1:T(8,128)S(1)} %convolution_bitcast_fusion.9, ...), kind=kOutput, calls=%fused_computation.134 | convolution fusion | flops 12275712 | bytes 5914724 | tf_op jit(solution)/shard_map/ec,exyz->cxyz/dot_general | solution.py:34
  50.1 0.0 copy-start.5
  50.2 1.0 copy.39
  51.2 1.9 %collective-permute-start.8 = (f32[5,1,16,256]{3,0,2,1:T(8,128)S(1)}, f32[5,1,16,256]{3,0,2,1:T(8,128)S(1)}, u32[]{:S(2)}, u32[]{:S(2)}) collective-permute-start(f32[5,1,16,256]{3,0,2,1:T(8,128)S(1)} %get-tuple-element.15), channel_id=1, source_target_pairs={{4,0},{8,4},{12,8},{5,1},{9,5},{13,9},{6,2},{10,6},{14,10},{7,3},{... | collective-permute-start | bytes 245768 | tf_op jit(solution)/shard_map/ppermute | solution.py:19
  53.1 2.4 %collective-permute-start.9 = (f32[5,1,16,256]{3,0,2,1:T(8,128)S(1)}, f32[5,1,16,256]{3,0,2,1:T(8,128)S(1)}, u32[]{:S(2)}, u32[]{:S(2)}) collective-permute-start(f32[5,1,16,256]{3,0,2,1:T(8,128)S(1)} %get-tuple-element.14), channel_id=1, source_target_pairs={{0,4},{4,8},{8,12},{1,5},{5,9},{9,13},{2,6},{6,10},{10,14},{3,7},{... | collective-permute-start | bytes 245768 | tf_op jit(solution)/shard_map/ppermute | solution.py:16
  55.6 0.3 fusion.158
  55.8 0.2 fusion.120
  56.0 0.1 fusion.156
  56.1 0.1 mul.57
  56.2 41.7 %psum.7 = f32[4096]{0:T(1024)S(1)} all-reduce(f32[4096]{0:T(1024)S(1)} %mul.57), channel_id=1, replica_groups=mesh['cond'=2,'gx'=4,'yz'=4] {'cond','gx','yz'}, use_global_device_ids=true, to_apply=%region_3.4 | all-reduce | flops 4096 | bytes 32768 | tf_op jit(solution)/shard_map/psum | solution.py:94
  97.9 0.6 dynamic_slice.3
  98.5 2.4 %collective-permute-start.10 = (f32[5,10,1,256]{3,0,2,1:T(8,128)S(1)}, f32[5,10,1,256]{3,0,2,1:T(8,128)S(1)}, u32[]{:S(2)}, u32[]{:S(2)}) collective-permute-start(f32[5,10,1,256]{3,0,2,1:T(8,128)S(1)} %get-tuple-element.9), channel_id=1, source_target_pairs={{1,0},{2,1},{3,2},{5,4},{6,5},{7,6},{9,8},{10,9},{11,10},{13,12},{... | collective-permute-start | bytes 153608 | tf_op jit(solution)/shard_map/ppermute | solution.py:19
  101.0 3.6 %collective-permute-start.11 = (f32[5,10,1,256]{3,0,2,1:T(8,128)S(1)}, f32[5,10,1,256]{3,0,2,1:T(8,128)S(1)}, u32[]{:S(2)}, u32[]{:S(2)}) collective-permute-start(f32[5,10,1,256]{3,0,2,1:T(8,128)S(1)} %get-tuple-element.8), channel_id=1, source_target_pairs={{0,1},{1,2},{2,3},{4,5},{5,6},{6,7},{8,9},{9,10},{10,11},{12,13},{... | collective-permute-start | bytes 153608 | tf_op jit(solution)/shard_map/ppermute | solution.py:16
  104.6 1.1 convolution_bitcast_fusion
  105.7 1.6 %collective-permute-done.11 = f32[5,10,1,256]{3,0,2,1:T(8,128)S(1)} collective-permute-done((f32[5,10,1,256]{3,0,2,1:T(8,128)S(1)}, f32[5,10,1,256]{3,0,2,1:T(8,128)S(1)}, u32[]{:S(2)}, u32[]{:S(2)}) %collective-permute-start.11) | collective-permute-done | bytes 51232 | tf_op jit(solution)/shard_map/ppermute | solution.py:16
  107.3 0.6 select_maximum_fusion
  108.0 1.0 convolution_bitcast_fusion.6
  109.0 1.2 %convolution_bitcast_fusion.7 = f32[5,8,16,256]{3,0,2,1:T(8,128)S(1)} fusion(f32[5,10,18,258]{3,0,2,1:T(8,128)S(1)} %select_maximum_fusion, f32[1,1,5,5]{3,2,1,0:T(8,128)S(1)} %copy.81), kind=kOutput, calls=%fused_computation.82 | convolution fusion | flops 9830400 | bytes 1708032 | tf_op jit(solution)/shard_map/ec,exyz->cxyz/dot_general | solution.py:34
  110.3 1.1 fusion.49
  111.3 1.1 fusion.52
  112.4 2.0 %fusion.86 = f32[1,5,8,16,256]{4,1,3,2,0:T(8,128)S(1)} fusion(f32[5,8,16,256]{3,0,2,1:T(8,128)S(1)} %convolution_bitcast_fusion.6, f32[5,8,16,256]{3,0,2,1:T(8,128)S(1)} %convolution_bitcast_fusion.7, f32[5,8,16,256]{3,0,2,1:T(8,128)S(1)} %fusion.49, f32[5,8,16,256]{3,0,2,1:T(8,128)S(1)} %fusion.52, f32[5,8,16,256]{3,0,2,1:T(8,128)S(1)} %convolution_bitcast_fusion, ...), kind=kOutput, calls=%fused_computation.100 | convolution fusion | flops 11325440 | bytes 5455972 | tf_op jit(solution)/shard_map/ec,exyz->cxyz/dot_general | solution.py:34
  114.4 1.0 copy.40
  (23 shorter events, 0.2 us)
Async XLA Ops:
  0.6 54.9 %copy-start = (f32[256,128]{1,0:T(8,128)S(1)}, f32[256,128]{1,0:T(8,128)}, u32[]{:S(2)}) copy-start(f32[256,128]{1,0:T(8,128)} %param.16) | copy-start | bytes 393220
  0.6 5.9 %copy-start.4 = (f32[1,6,5,5]{1,0,3,2:T(1,128)S(1)}, f32[1,6,5,5]{1,0,3,2:T(1,128)}, u32[]{:S(2)}) copy-start(f32[1,6,5,5]{1,0,3,2:T(1,128)} %param.12) | copy-start | bytes 1804
  0.7 6.9 %copy-start.6 = (s32[8,16]{1,0:T(8,128)S(1)}, s32[8,16]{1,0:T(8,128)}, u32[]{:S(2)}) copy-start(s32[8,16]{1,0:T(8,128)} %param.15) | copy-start | bytes 1540
  2.2 5.4 %collective-permute-start = (f32[5,1,16,256]{3,0,2,1:T(8,128)S(1)}, f32[5,1,16,256]{3,0,2,1:T(8,128)S(1)}, u32[]{:S(2)}, u32[]{:S(2)}) collective-permute-start(f32[5,1,16,256]{3,0,2,1:T(8,128)S(1)} %get-tuple-element.19), channel_id=1, source_target_pairs={{4,0},{8,4},{12,8},{5,1},{9,5},{13,9},{6,2},{10,6},{14,10},{7,3},{... | collective-permute-start | bytes 245768 | tf_op jit(solution)/shard_map/ppermute | solution.py:19
  4.1 6.3 %collective-permute-start.1 = (f32[5,1,16,256]{3,0,2,1:T(8,128)S(1)}, f32[5,1,16,256]{3,0,2,1:T(8,128)S(1)}, u32[]{:S(2)}, u32[]{:S(2)}) collective-permute-start(f32[5,1,16,256]{3,0,2,1:T(8,128)S(1)} %get-tuple-element.18), channel_id=1, source_target_pairs={{0,4},{4,8},{8,12},{1,5},{5,9},{9,13},{2,6},{6,10},{10,14},{3,7},{... | collective-permute-start | bytes 245768 | tf_op jit(solution)/shard_map/ppermute | solution.py:16
  10.4 6.9 %collective-permute-start.2 = (f32[5,10,1,256]{3,0,2,1:T(8,128)S(1)}, f32[5,10,1,256]{3,0,2,1:T(8,128)S(1)}, u32[]{:S(2)}, u32[]{:S(2)}) collective-permute-start(f32[5,10,1,256]{3,0,2,1:T(8,128)S(1)} %get-tuple-element.13), channel_id=1, source_target_pairs={{1,0},{2,1},{3,2},{5,4},{6,5},{7,6},{9,8},{10,9},{11,10},{13,12},{... | collective-permute-start | bytes 153608 | tf_op jit(solution)/shard_map/ppermute | solution.py:19
  12.8 6.3 %collective-permute-start.3 = (f32[5,10,1,256]{3,0,2,1:T(8,128)S(1)}, f32[5,10,1,256]{3,0,2,1:T(8,128)S(1)}, u32[]{:S(2)}, u32[]{:S(2)}) collective-permute-start(f32[5,10,1,256]{3,0,2,1:T(8,128)S(1)} %get-tuple-element.12), channel_id=1, source_target_pairs={{0,1},{1,2},{2,3},{4,5},{5,6},{6,7},{8,9},{9,10},{10,11},{12,13},{... | collective-permute-start | bytes 153608 | tf_op jit(solution)/shard_map/ppermute | solution.py:16
  22.1 2.2 %copy-start.1 = (f32[1,5,8,16,256]{4,3,2,1,0:T(8,128)S(1)}, f32[1,5,8,16,256]{4,3,2,1,0:T(8,128)}, u32[]{:S(2)}) copy-start(f32[1,5,8,16,256]{4,3,2,1,0:T(8,128)} %param.10) | copy-start | bytes 1966084
  22.1 2.2 %copy-start.2 = (f32[8,16,256]{2,1,0:T(8,128)S(1)}, f32[8,16,256]{2,1,0:T(8,128)}, u32[]{:S(2)}) copy-start(f32[8,16,256]{2,1,0:T(8,128)} %param.11) | copy-start | bytes 393220
  24.3 6.4 %copy-start.7 = (s32[2]{0:T(128)S(1)}, s32[2]{0:T(128)}, u32[]{:S(2)}) copy-start(s32[2]{0:T(128)} %param.17) | copy-start | bytes 28
  26.3 6.3 %collective-permute-start.4 = (f32[5,1,16,256]{3,0,2,1:T(8,128)S(1)}, f32[5,1,16,256]{3,0,2,1:T(8,128)S(1)}, u32[]{:S(2)}, u32[]{:S(2)}) collective-permute-start(f32[5,1,16,256]{3,0,2,1:T(8,128)S(1)} %get-tuple-element.17), channel_id=1, source_target_pairs={{4,0},{8,4},{12,8},{5,1},{9,5},{13,9},{6,2},{10,6},{14,10},{7,3},{... | collective-permute-start | bytes 245768 | tf_op jit(solution)/shard_map/ppermute | solution.py:19
  28.3 6.3 %collective-permute-start.5 = (f32[5,1,16,256]{3,0,2,1:T(8,128)S(1)}, f32[5,1,16,256]{3,0,2,1:T(8,128)S(1)}, u32[]{:S(2)}, u32[]{:S(2)}) collective-permute-start(f32[5,1,16,256]{3,0,2,1:T(8,128)S(1)} %get-tuple-element.16), channel_id=1, source_target_pairs={{0,4},{4,8},{8,12},{1,5},{5,9},{9,13},{2,6},{6,10},{10,14},{3,7},{... | collective-permute-start | bytes 245768 | tf_op jit(solution)/shard_map/ppermute | solution.py:16
  34.6 7.1 %collective-permute-start.6 = (f32[5,10,1,256]{3,0,2,1:T(8,128)S(1)}, f32[5,10,1,256]{3,0,2,1:T(8,128)S(1)}, u32[]{:S(2)}, u32[]{:S(2)}) collective-permute-start(f32[5,10,1,256]{3,0,2,1:T(8,128)S(1)} %get-tuple-element.11), channel_id=1, source_target_pairs={{1,0},{2,1},{3,2},{5,4},{6,5},{7,6},{9,8},{10,9},{11,10},{13,12},{... | collective-permute-start | bytes 153608 | tf_op jit(solution)/shard_map/ppermute | solution.py:19
  36.5 6.3 %collective-permute-start.7 = (f32[5,10,1,256]{3,0,2,1:T(8,128)S(1)}, f32[5,10,1,256]{3,0,2,1:T(8,128)S(1)}, u32[]{:S(2)}, u32[]{:S(2)}) collective-permute-start(f32[5,10,1,256]{3,0,2,1:T(8,128)S(1)} %get-tuple-element.10), channel_id=1, source_target_pairs={{0,1},{1,2},{2,3},{4,5},{5,6},{6,7},{8,9},{9,10},{10,11},{12,13},{... | collective-permute-start | bytes 153608 | tf_op jit(solution)/shard_map/ppermute | solution.py:16
  45.8 2.2 %copy-start.3 = (bf16[1,5,8,16,256]{4,3,2,1,0:T(8,128)(2,1)S(1)}, bf16[1,5,8,16,256]{4,3,2,1,0:T(8,128)(2,1)}, u32[]{:S(2)}) copy-start(bf16[1,5,8,16,256]{4,3,2,1,0:T(8,128)(2,1)} %param.13) | copy-start | bytes 983044
  50.1 5.4 %copy-start.5 = (s32[8,16,256]{2,1,0:T(8,128)S(1)}, s32[8,16,256]{2,1,0:T(8,128)}, u32[]{:S(2)}) copy-start(s32[8,16,256]{2,1,0:T(8,128)} %param.14) | copy-start | bytes 393220
  51.2 47.3 %collective-permute-start.8 = (f32[5,1,16,256]{3,0,2,1:T(8,128)S(1)}, f32[5,1,16,256]{3,0,2,1:T(8,128)S(1)}, u32[]{:S(2)}, u32[]{:S(2)}) collective-permute-start(f32[5,1,16,256]{3,0,2,1:T(8,128)S(1)} %get-tuple-element.15), channel_id=1, source_target_pairs={{4,0},{8,4},{12,8},{5,1},{9,5},{13,9},{6,2},{10,6},{14,10},{7,3},{... | collective-permute-start | bytes 245768 | tf_op jit(solution)/shard_map/ppermute | solution.py:19
  53.1 45.4 %collective-permute-start.9 = (f32[5,1,16,256]{3,0,2,1:T(8,128)S(1)}, f32[5,1,16,256]{3,0,2,1:T(8,128)S(1)}, u32[]{:S(2)}, u32[]{:S(2)}) collective-permute-start(f32[5,1,16,256]{3,0,2,1:T(8,128)S(1)} %get-tuple-element.14), channel_id=1, source_target_pairs={{0,4},{4,8},{8,12},{1,5},{5,9},{9,13},{2,6},{6,10},{10,14},{3,7},{... | collective-permute-start | bytes 245768 | tf_op jit(solution)/shard_map/ppermute | solution.py:16
  98.5 7.2 %collective-permute-start.10 = (f32[5,10,1,256]{3,0,2,1:T(8,128)S(1)}, f32[5,10,1,256]{3,0,2,1:T(8,128)S(1)}, u32[]{:S(2)}, u32[]{:S(2)}) collective-permute-start(f32[5,10,1,256]{3,0,2,1:T(8,128)S(1)} %get-tuple-element.9), channel_id=1, source_target_pairs={{1,0},{2,1},{3,2},{5,4},{6,5},{7,6},{9,8},{10,9},{11,10},{13,12},{... | collective-permute-start | bytes 153608 | tf_op jit(solution)/shard_map/ppermute | solution.py:19
  101.0 6.3 %collective-permute-start.11 = (f32[5,10,1,256]{3,0,2,1:T(8,128)S(1)}, f32[5,10,1,256]{3,0,2,1:T(8,128)S(1)}, u32[]{:S(2)}, u32[]{:S(2)}) collective-permute-start(f32[5,10,1,256]{3,0,2,1:T(8,128)S(1)} %get-tuple-element.8), channel_id=1, source_target_pairs={{0,1},{1,2},{2,3},{4,5},{5,6},{6,7},{8,9},{9,10},{10,11},{12,13},{... | collective-permute-start | bytes 153608 | tf_op jit(solution)/shard_map/ppermute | solution.py:16
where the time goes:
time: 116 us; the launch traced here: 115 us
  blocking collectives  41.7 us (36%)
  starting transfers between devices  30.9 us (27%)
  matrix products  23 us (20%)
  waiting for transfers between devices  9.19 us (8%)
  local copies, waits for them, and re-layouts  5.56 us (5%)
  other arithmetic  2.64 us (2%)
  between operations  2.47 us (2%)
    psum x1, blocking collectives, local(): summed = lax.psum(local_portion * gradient, ('cond', 'gx', 'yz'))  41.7 us
    dot_general x18, matrix products, apply_operator(): jnp.einsum('ec,exyz->cxyz', blocks[direction], shifted, precision=lax.Pre...  22.6 us
    ppermute x6, starting transfers between devices, with_halo(): lax.ppermute(lax.slice_in_dim(block, block.shape[dim] - width, None, axis...  18.4 us
    ppermute x6, starting transfers between devices, with_halo(): lax.ppermute(lax.slice_in_dim(block, 0, width, axis=dim), axis, backward)  12.5 us
    ppermute x6, waiting for transfers between devices, with_halo(): lax.ppermute(lax.slice_in_dim(block, block.shape[dim] - width, None, axis...  9.18 us
    unnamed x25, local copies, waits for them, and re-layouts  4.43 us
  transfers between devices with their start and end apart: 12, of which 5 were waited for; matrix products, arithmetic and copies ran while one was open for 5% of the time, Pallas kernels for 0%

commit v1 on v0

--- a/solution.py
+++ b/solution.py
@@ -91,7 +91,9 @@
     weights_float = condition_weights.astype(jnp.float32)
     picked = jnp.arange(weights_float.shape[0]) == lax.axis_index("cond")
     local_portion = jnp.sum(jnp.where(picked, weights_float, 0.0)) / jnp.sum(weights_float)
-    summed = lax.psum(local_portion * gradient, ("cond", "gx", "yz"))
+    block_2 = local_portion * gradient
+    shards = lax.all_gather(block_2, ("cond", "gx", "yz"))
+    summed = jnp.sum(shards, axis=0)
     pieces = NDES // lax.axis_size(("gx", "yz"))
     design_gradient = lax.dynamic_slice_in_dim(
         summed, lax.axis_index(("gx", "yz")) * pieces, pieces, 0

time: 116 us -> 148 us (1.28)
  the two profiles are of different devices: /device:TPU:12 before, /device:TPU:0 now
where the time goes in v1:
time: 148 us
  blocking collectives  75.7 us (51%)
  starting transfers between devices  35.3 us (24%)
  matrix products  23 us (16%)
  local copies, waits for them, and re-layouts  5.57 us (4%)
  other arithmetic  2.99 us (2%)
  between operations  2.49 us (2%)
  waiting for transfers between devices  2.47 us (2%)
    all_gather x1, blocking collectives, local(): shards = lax.all_gather(block_2, ('cond', 'gx', 'yz'))  75.7 us
    ppermute x6, starting transfers between devices, with_halo(): lax.ppermute(lax.slice_in_dim(block, block.shape[dim] - width, None, axis...  27.6 us
    dot_general x18, matrix products, apply_operator(): jnp.einsum('ec,exyz->cxyz', blocks[direction], shifted, precision=lax.Pre...  22.6 us
    ppermute x6, starting transfers between devices, with_halo(): lax.ppermute(lax.slice_in_dim(block, 0, width, axis=dim), axis, backward)  7.75 us
    unnamed x26, local copies, waits for them, and re-layouts  4.51 us
  transfers between devices with their start and end apart: 12, of which 3 were waited for; matrix products, arithmetic and copies ran while one was open for 5% of the time, Pallas kernels for 0%

profile of v1, /device:TPU:0, one launch (start us, length us, event | category | flops | bytes accessed | tf_op | source)
XLA Modules:
  0.0 147.6 jit_solution(14625260624071816642)
XLA Ops:
  0.6 0.0 copy-start
  0.7 1.5 %copy.117 = f32[1,5,8,16,256]{4,1,3,2,0:T(8,128)S(1)} copy(f32[1,5,8,16,256]{4,3,2,1,0:T(8,128)} %param.9) | data formatting | bytes 1310720 | tf_op args[0]
  2.2 1.3 collective-permute-start
  3.5 3.0 %collective-permute-start.1 = (f32[5,1,16,256]{3,0,2,1:T(8,128)S(1)}, f32[5,1,16,256]{3,0,2,1:T(8,128)S(1)}, u32[]{:S(2)}, u32[]{:S(2)}) collective-permute-start(f32[5,1,16,256]{3,0,2,1:T(8,128)S(1)} %get-tuple-element.21), channel_id=1, source_target_pairs={{0,4},{4,8},{8,12},{1,5},{5,9},{9,13},{2,6},{6,10},{10,14},{3,7},{... | collective-permute-start | bytes 245768 | tf_op jit(solution)/shard_map/ppermute | solution.py:16
  6.6 0.2 fusion.157
  6.8 0.1 copy.111
  6.9 0.1 copy.110
  7.0 0.1 copy.109
  7.2 0.1 copy.108
  7.3 0.1 copy.107
  7.4 0.1 copy.106
  7.6 0.1 eq.24
  7.6 0.0 collective-permute-done
  7.7 0.0 collective-permute-done.1
  7.7 1.3 collective-permute-start.2
  9.0 5.6 %collective-permute-start.3 = (f32[5,10,1,256]{3,0,2,1:T(8,128)S(1)}, f32[5,10,1,256]{3,0,2,1:T(8,128)S(1)}, u32[]{:S(2)}, u32[]{:S(2)}) collective-permute-start(f32[5,10,1,256]{3,0,2,1:T(8,128)S(1)} %get-tuple-element.15), channel_id=1, source_target_pairs={{0,1},{1,2},{2,3},{4,5},{5,6},{6,7},{8,9},{9,10},{10,11},{12,13},{... | collective-permute-start | bytes 153608 | tf_op jit(solution)/shard_map/ppermute | solution.py:16
  14.6 1.1 convolution_bitcast_fusion.4
  15.7 0.9 collective-permute-done.3
  16.6 0.6 select_maximum_fusion.8
  17.3 1.0 convolution_bitcast_fusion.10
  18.3 1.2 convolution_bitcast_fusion.11
  19.6 0.0 copy-start.1
  19.6 0.0 copy-start.2
  19.6 1.1 fusion.61
  20.7 1.1 fusion.64
  21.8 0.0 copy-start.7
  21.8 2.0 %fusion.94 = f32[5,8,16,256]{3,0,2,1:T(8,128)S(1)} fusion(f32[5,8,16,256]{3,0,2,1:T(8,128)S(1)} %bitcast.184, f32[5,8,16,256]{3,0,2,1:T(8,128)S(1)} %convolution_bitcast_fusion.10, f32[5,8,16,256]{3,0,2,1:T(8,128)S(1)} %convolution_bitcast_fusion.11, f32[5,8,16,256]{3,0,2,1:T(8,128)S(1)} %fusion.61, f32[5,8,16,256]{3,0,2,1:T(8,128)S(1)} %fusion.64, ...), kind=kOutput, calls=%fused_computation.108 | convolution fusion | flops 11816960 | bytes 5455972 | tf_op jit(solution)/shard_map/ec,exyz->cxyz/dot_general | solution.py:34
  23.8 1.3 collective-permute-start.4
  25.1 3.8 %collective-permute-start.5 = (f32[5,1,16,256]{3,0,2,1:T(8,128)S(1)}, f32[5,1,16,256]{3,0,2,1:T(8,128)S(1)}, u32[]{:S(2)}, u32[]{:S(2)}) collective-permute-start(f32[5,1,16,256]{3,0,2,1:T(8,128)S(1)} %get-tuple-element.19), channel_id=1, source_target_pairs={{0,4},{4,8},{8,12},{1,5},{5,9},{9,13},{2,6},{6,10},{10,14},{3,7},{... | collective-permute-start | bytes 245768 | tf_op jit(solution)/shard_map/ppermute | solution.py:16
  28.9 0.6 convert_reduce_fusion
  30.9 0.0 collective-permute-done.5
  30.9 1.3 collective-permute-start.6
  32.2 4.8 %collective-permute-start.7 = (f32[5,10,1,256]{3,0,2,1:T(8,128)S(1)}, f32[5,10,1,256]{3,0,2,1:T(8,128)S(1)}, u32[]{:S(2)}, u32[]{:S(2)}) collective-permute-start(f32[5,10,1,256]{3,0,2,1:T(8,128)S(1)} %get-tuple-element.13), channel_id=1, source_target_pairs={{0,1},{1,2},{2,3},{4,5},{5,6},{6,7},{8,9},{9,10},{10,11},{12,13},{... | collective-permute-start | bytes 153608 | tf_op jit(solution)/shard_map/ppermute | solution.py:16
  37.0 1.1 convolution_bitcast_fusion.2
  38.1 0.8 collective-permute-done.7
  38.9 0.6 select_maximum_fusion.4
  39.5 1.0 convolution_bitcast_fusion.8
  40.6 1.2 convolution_bitcast_fusion.9
  41.8 0.0 copy-start.3
  41.8 1.1 fusion.55
  42.9 1.1 fusion.58
  44.0 0.0 copy-start.5
  44.0 2.2 %fusion.119 = (f32[8,16,256]{2,1,0:T(8,128)S(1)}, f32[5,8,16,256]{3,0,2,1:T(8,128)S(1)}) fusion(bf16[1,5,8,16,256]{4,3,2,1,0:T(8,128)(2,1)S(1)} %copy-done.3, f32[5,8,16,256]{3,0,2,1:T(8,128)S(1)} %fusion.94, f32[5,8,16,256]{3,0,2,1:T(8,128)S(1)} %convolution_bitcast_fusion.8, f32[5,8,16,256]{3,0,2,1:T(8,128)S(1)} %convolution_bitcast_fusion.9, ...), kind=kOutput, calls=%fused_computation.134 | convolution fusion | flops 12275712 | bytes 5914724 | tf_op jit(solution)/shard_map/ec,exyz->cxyz/dot_general | solution.py:34
  46.2 1.3 collective-permute-start.8
  47.5 5.6 %collective-permute-start.9 = (f32[5,1,16,256]{3,0,2,1:T(8,128)S(1)}, f32[5,1,16,256]{3,0,2,1:T(8,128)S(1)}, u32[]{:S(2)}, u32[]{:S(2)}) collective-permute-start(f32[5,1,16,256]{3,0,2,1:T(8,128)S(1)} %get-tuple-element.17), channel_id=1, source_target_pairs={{0,4},{4,8},{8,12},{1,5},{5,9},{9,13},{2,6},{6,10},{10,14},{3,7},{... | collective-permute-start | bytes 245768 | tf_op jit(solution)/shard_map/ppermute | solution.py:16
  53.1 0.3 fusion.158
  53.4 0.2 fusion.120
  53.6 0.1 fusion.156
  53.7 0.1 reshape.41
  53.7 75.7 %all-gather = f32[32,1,4096]{2,1,0:T(1,128)S(1)} all-gather(f32[1,1,4096]{2,1,0:T(1,128)S(1)} %reshape.41), channel_id=1, replica_groups=mesh['cond'=2,'gx'=4,'yz'=4] {'cond','gx','yz'}, dimensions={0}, use_global_device_ids=true | all-gather | bytes 540672 | tf_op jit(solution)/shard_map/all_gather | solution.py:95
  129.5 1.0 copy.68
  130.5 0.4 reduce_sum.39
  130.9 0.6 dynamic_slice.3
  131.5 1.3 collective-permute-start.10
  132.8 4.8 %collective-permute-start.11 = (f32[5,10,1,256]{3,0,2,1:T(8,128)S(1)}, f32[5,10,1,256]{3,0,2,1:T(8,128)S(1)}, u32[]{:S(2)}, u32[]{:S(2)}) collective-permute-start(f32[5,10,1,256]{3,0,2,1:T(8,128)S(1)} %get-tuple-element.11), channel_id=1, source_target_pairs={{0,1},{1,2},{2,3},{4,5},{5,6},{6,7},{8,9},{9,10},{10,11},{12,13},{... | collective-permute-start | bytes 153608 | tf_op jit(solution)/shard_map/ppermute | solution.py:16
  137.6 1.1 convolution_bitcast_fusion
  138.7 0.7 collective-permute-done.11
  139.4 0.6 select_maximum_fusion
  140.1 1.0 convolution_bitcast_fusion.6
  141.1 1.2 convolution_bitcast_fusion.7
  142.4 1.1 fusion.49
  143.5 1.1 fusion.52
  144.5 2.0 %fusion.86 = f32[1,5,8,16,256]{4,1,3,2,0:T(8,128)S(1)} fusion(f32[5,8,16,256]{3,0,2,1:T(8,128)S(1)} %convolution_bitcast_fusion.6, f32[5,8,16,256]{3,0,2,1:T(8,128)S(1)} %convolution_bitcast_fusion.7, f32[5,8,16,256]{3,0,2,1:T(8,128)S(1)} %fusion.49, f32[5,8,16,256]{3,0,2,1:T(8,128)S(1)} %fusion.52, f32[5,8,16,256]{3,0,2,1:T(8,128)S(1)} %convolution_bitcast_fusion, ...), kind=kOutput, calls=%fused_computation.100 | convolution fusion | flops 11325440 | bytes 5455972 | tf_op jit(solution)/shard_map/ec,exyz->cxyz/dot_general | solution.py:34
  146.5 1.0 copy.69
  (24 shorter events, 0.2 us)
Async XLA Ops:
  0.6 52.5 %copy-start = (f32[256,128]{1,0:T(8,128)S(1)}, f32[256,128]{1,0:T(8,128)}, u32[]{:S(2)}) copy-start(f32[256,128]{1,0:T(8,128)} %param.16) | copy-start | bytes 393220
  0.6 5.9 %copy-start.4 = (f32[1,6,5,5]{1,0,3,2:T(1,128)S(1)}, f32[1,6,5,5]{1,0,3,2:T(1,128)}, u32[]{:S(2)}) copy-start(f32[1,6,5,5]{1,0,3,2:T(1,128)} %param.12) | copy-start | bytes 1804
  0.7 6.9 %copy-start.6 = (s32[8,16]{1,0:T(8,128)S(1)}, s32[8,16]{1,0:T(8,128)}, u32[]{:S(2)}) copy-start(s32[8,16]{1,0:T(8,128)} %param.15) | copy-start | bytes 1540
  2.2 5.4 %collective-permute-start = (f32[5,1,16,256]{3,0,2,1:T(8,128)S(1)}, f32[5,1,16,256]{3,0,2,1:T(8,128)S(1)}, u32[]{:S(2)}, u32[]{:S(2)}) collective-permute-start(f32[5,1,16,256]{3,0,2,1:T(8,128)S(1)} %get-tuple-element.22), channel_id=1, source_target_pairs={{4,0},{8,4},{12,8},{5,1},{9,5},{13,9},{6,2},{10,6},{14,10},{7,3},{... | collective-permute-start | bytes 245768 | tf_op jit(solution)/shard_map/ppermute | solution.py:19
  3.5 4.2 %collective-permute-start.1 = (f32[5,1,16,256]{3,0,2,1:T(8,128)S(1)}, f32[5,1,16,256]{3,0,2,1:T(8,128)S(1)}, u32[]{:S(2)}, u32[]{:S(2)}) collective-permute-start(f32[5,1,16,256]{3,0,2,1:T(8,128)S(1)} %get-tuple-element.21), channel_id=1, source_target_pairs={{0,4},{4,8},{8,12},{1,5},{5,9},{9,13},{2,6},{6,10},{10,14},{3,7},{... | collective-permute-start | bytes 245768 | tf_op jit(solution)/shard_map/ppermute | solution.py:16
  7.7 8.0 %collective-permute-start.2 = (f32[5,10,1,256]{3,0,2,1:T(8,128)S(1)}, f32[5,10,1,256]{3,0,2,1:T(8,128)S(1)}, u32[]{:S(2)}, u32[]{:S(2)}) collective-permute-start(f32[5,10,1,256]{3,0,2,1:T(8,128)S(1)} %get-tuple-element.16), channel_id=1, source_target_pairs={{1,0},{2,1},{3,2},{5,4},{6,5},{7,6},{9,8},{10,9},{11,10},{13,12},{... | collective-permute-start | bytes 153608 | tf_op jit(solution)/shard_map/ppermute | solution.py:19
  9.0 7.6 %collective-permute-start.3 = (f32[5,10,1,256]{3,0,2,1:T(8,128)S(1)}, f32[5,10,1,256]{3,0,2,1:T(8,128)S(1)}, u32[]{:S(2)}, u32[]{:S(2)}) collective-permute-start(f32[5,10,1,256]{3,0,2,1:T(8,128)S(1)} %get-tuple-element.15), channel_id=1, source_target_pairs={{0,1},{1,2},{2,3},{4,5},{5,6},{6,7},{8,9},{9,10},{10,11},{12,13},{... | collective-permute-start | bytes 153608 | tf_op jit(solution)/shard_map/ppermute | solution.py:16
  19.6 2.2 %copy-start.1 = (f32[1,5,8,16,256]{4,3,2,1,0:T(8,128)S(1)}, f32[1,5,8,16,256]{4,3,2,1,0:T(8,128)}, u32[]{:S(2)}) copy-start(f32[1,5,8,16,256]{4,3,2,1,0:T(8,128)} %param.10) | copy-start | bytes 1966084
  19.6 2.2 %copy-start.2 = (f32[8,16,256]{2,1,0:T(8,128)S(1)}, f32[8,16,256]{2,1,0:T(8,128)}, u32[]{:S(2)}) copy-start(f32[8,16,256]{2,1,0:T(8,128)} %param.11) | copy-start | bytes 393220
  21.8 7.2 %copy-start.7 = (s32[2]{0:T(128)S(1)}, s32[2]{0:T(128)}, u32[]{:S(2)}) copy-start(s32[2]{0:T(128)} %param.17) | copy-start | bytes 28
  23.8 7.1 %collective-permute-start.4 = (f32[5,1,16,256]{3,0,2,1:T(8,128)S(1)}, f32[5,1,16,256]{3,0,2,1:T(8,128)S(1)}, u32[]{:S(2)}, u32[]{:S(2)}) collective-permute-start(f32[5,1,16,256]{3,0,2,1:T(8,128)S(1)} %get-tuple-element.20), channel_id=1, source_target_pairs={{4,0},{8,4},{12,8},{5,1},{9,5},{13,9},{6,2},{10,6},{14,10},{7,3},{... | collective-permute-start | bytes 245768 | tf_op jit(solution)/shard_map/ppermute | solution.py:19
  25.1 5.8 %collective-permute-start.5 = (f32[5,1,16,256]{3,0,2,1:T(8,128)S(1)}, f32[5,1,16,256]{3,0,2,1:T(8,128)S(1)}, u32[]{:S(2)}, u32[]{:S(2)}) collective-permute-start(f32[5,1,16,256]{3,0,2,1:T(8,128)S(1)} %get-tuple-element.19), channel_id=1, source_target_pairs={{0,4},{4,8},{8,12},{1,5},{5,9},{9,13},{2,6},{6,10},{10,14},{3,7},{... | collective-permute-start | bytes 245768 | tf_op jit(solution)/shard_map/ppermute | solution.py:16
  30.9 7.2 %collective-permute-start.6 = (f32[5,10,1,256]{3,0,2,1:T(8,128)S(1)}, f32[5,10,1,256]{3,0,2,1:T(8,128)S(1)}, u32[]{:S(2)}, u32[]{:S(2)}) collective-permute-start(f32[5,10,1,256]{3,0,2,1:T(8,128)S(1)} %get-tuple-element.14), channel_id=1, source_target_pairs={{1,0},{2,1},{3,2},{5,4},{6,5},{7,6},{9,8},{10,9},{11,10},{13,12},{... | collective-permute-start | bytes 153608 | tf_op jit(solution)/shard_map/ppermute | solution.py:19
  32.2 6.7 %collective-permute-start.7 = (f32[5,10,1,256]{3,0,2,1:T(8,128)S(1)}, f32[5,10,1,256]{3,0,2,1:T(8,128)S(1)}, u32[]{:S(2)}, u32[]{:S(2)}) collective-permute-start(f32[5,10,1,256]{3,0,2,1:T(8,128)S(1)} %get-tuple-element.13), channel_id=1, source_target_pairs={{0,1},{1,2},{2,3},{4,5},{5,6},{6,7},{8,9},{9,10},{10,11},{12,13},{... | collective-permute-start | bytes 153608 | tf_op jit(solution)/shard_map/ppermute | solution.py:16
  41.8 2.2 %copy-start.3 = (bf16[1,5,8,16,256]{4,3,2,1,0:T(8,128)(2,1)S(1)}, bf16[1,5,8,16,256]{4,3,2,1,0:T(8,128)(2,1)}, u32[]{:S(2)}) copy-start(bf16[1,5,8,16,256]{4,3,2,1,0:T(8,128)(2,1)} %param.13) | copy-start | bytes 983044
  44.0 9.1 %copy-start.5 = (s32[8,16,256]{2,1,0:T(8,128)S(1)}, s32[8,16,256]{2,1,0:T(8,128)}, u32[]{:S(2)}) copy-start(s32[8,16,256]{2,1,0:T(8,128)} %param.14) | copy-start | bytes 393220
  46.2 85.3 %collective-permute-start.8 = (f32[5,1,16,256]{3,0,2,1:T(8,128)S(1)}, f32[5,1,16,256]{3,0,2,1:T(8,128)S(1)}, u32[]{:S(2)}, u32[]{:S(2)}) collective-permute-start(f32[5,1,16,256]{3,0,2,1:T(8,128)S(1)} %get-tuple-element.18), channel_id=1, source_target_pairs={{4,0},{8,4},{12,8},{5,1},{9,5},{13,9},{6,2},{10,6},{14,10},{7,3},{... | collective-permute-start | bytes 245768 | tf_op jit(solution)/shard_map/ppermute | solution.py:19
  47.5 84.0 %collective-permute-start.9 = (f32[5,1,16,256]{3,0,2,1:T(8,128)S(1)}, f32[5,1,16,256]{3,0,2,1:T(8,128)S(1)}, u32[]{:S(2)}, u32[]{:S(2)}) collective-permute-start(f32[5,1,16,256]{3,0,2,1:T(8,128)S(1)} %get-tuple-element.17), channel_id=1, source_target_pairs={{0,4},{4,8},{8,12},{1,5},{5,9},{9,13},{2,6},{6,10},{10,14},{3,7},{... | collective-permute-start | bytes 245768 | tf_op jit(solution)/shard_map/ppermute | solution.py:16
  131.5 7.2 %collective-permute-start.10 = (f32[5,10,1,256]{3,0,2,1:T(8,128)S(1)}, f32[5,10,1,256]{3,0,2,1:T(8,128)S(1)}, u32[]{:S(2)}, u32[]{:S(2)}) collective-permute-start(f32[5,10,1,256]{3,0,2,1:T(8,128)S(1)} %get-tuple-element.12), channel_id=1, source_target_pairs={{1,0},{2,1},{3,2},{5,4},{6,5},{7,6},{9,8},{10,9},{11,10},{13,12},{... | collective-permute-start | bytes 153608 | tf_op jit(solution)/shard_map/ppermute | solution.py:19
  132.8 6.6 %collective-permute-start.11 = (f32[5,10,1,256]{3,0,2,1:T(8,128)S(1)}, f32[5,10,1,256]{3,0,2,1:T(8,128)S(1)}, u32[]{:S(2)}, u32[]{:S(2)}) collective-permute-start(f32[5,10,1,256]{3,0,2,1:T(8,128)S(1)} %get-tuple-element.11), channel_id=1, source_target_pairs={{0,1},{1,2},{2,3},{4,5},{5,6},{6,7},{8,9},{9,10},{10,11},{12,13},{... | collective-permute-start | bytes 153608 | tf_op jit(solution)/shard_map/ppermute | solution.py:16
